TPU v7x, 32 devices: a whole 2x2x4 slice. The times are simulated.
32 devices in a mesh: tm: 16 (over z, y, core), asset: 2 (over x).
Axes of the slice: x: 2, y: 2, z: 4, core: 2. Of those that a mesh axis runs over, the one named last changes fastest.
Arguments:
- tick_bars: float32 [2, 16, 61440], P('asset', 'tm'), may hold values from -20 to 20
- prior_bars: float32 [2, 16, 6400], P('asset', 'tm'), may hold values from -20 to 20, as said below
Outputs:
- connectedness: float32 [48, 8192], P('tm', 'asset')
Inputs may be any that keep to these rules, and one draw needn't show every extreme that they name: `prior_bars`: bar returns of the same assets.
All inputs are finite; a program needn't handle non-finite values.
Results may differ from a plain program's by a relative error of at most 0.0014.
Values may be sent and summed in bfloat16 or wider, within the bound.
A program may use at most 64 MiB of HBM per device.

v0:
```python
import functools
import math

import jax
import jax.numpy as jnp
from jax import lax
from jax.experimental import pallas as pl
from jax.experimental.pallas import tpu as pltpu
from jax.sharding import PartitionSpec as P

ASSETS = 8192
SPAN = 30
STRIDE = 5
WIN_DEV = 3
LEAD = 25
DEPTH = 32
TILE = 256
LANES = 128
SUBLANES = 8
PART_SCALE = 256.0


FLOOR_SQUARES = 1.0


def cycle_next(time, tile):
    core = time % 2
    along = (1 + core + tile) % 2
    return time + along * (1 - 2 * core), tile + (1 - along) * (1 - 2 * tile)


def around(block, forward):
    times, tiles = lax.axis_size("tm"), lax.axis_size("asset")
    route = []
    for time in range(times):
        for tile in range(tiles):
            next_time, next_tile = cycle_next(time, tile)
            hop = (time * tiles + tile, next_time * tiles + next_tile)
            route.append(hop if forward else hop[::-1])
    return lax.ppermute(block, ("tm", "asset"), route)


def window_stack(extended):
    columns = extended.shape[1]
    count = (extended.shape[0] - SPAN) // STRIDE + 1
    groups = extended.reshape(-1, STRIDE, columns)
    stacked = jnp.stack(
        [groups[offset : offset + count] for offset in range(SPAN // STRIDE)], axis=1
    )
    values = stacked.reshape(count, SPAN, columns)
    centred = values - jnp.mean(values, axis=1, keepdims=True)
    squares = jnp.sum(centred * centred, axis=1, keepdims=True)
    scaled = (centred * lax.rsqrt(jnp.maximum(squares, FLOOR_SQUARES))).astype(jnp.bfloat16)
    return jnp.pad(scaled, ((0, 0), (0, DEPTH - SPAN), (0, 0)))


def split_parts(block):
    scaled = block.astype(jnp.float32) * PART_SCALE
    high = scaled.astype(jnp.float8_e4m3fn).astype(jnp.float32)
    return high, scaled - high


def right_parts(block):
    high, low = split_parts(block)
    return jnp.concatenate([high, high, low, low], axis=0).astype(jnp.float8_e4m3fn)


def strip_totals(rows, source, first, count, column_sums, own_first):
    groups, _, width = source.shape
    high, low = split_parts(rows)
    rows_t = jnp.concatenate([high, low, high, low], axis=0).T.astype(jnp.float8_e4m3fn)
    row_partial = jnp.zeros((width, LANES), jnp.float32)
    for offset in range(count):
        group = lax.rem(first + offset, groups)
        magnitude = jnp.abs(jnp.dot(rows_t, source[group], preferred_element_type=jnp.float32))
        for lane in range(0, width, LANES):
            row_partial = row_partial + magnitude[:, lane : lane + LANES]
        if offset or not own_first:
            folded = jnp.sum(magnitude.reshape(width // SUBLANES, SUBLANES, width), axis=0)
            column_sums[group] = column_sums[group] + folded
    return jnp.sum(row_partial.T, axis=0, keepdims=True)


def fill_parts(source, parts):
    def fill(group, carry):
        parts[group] = right_parts(source[group])
        return carry

    lax.fori_loop(0, source.shape[0], fill, 0)


def diagonal(source, out, column_sums, parts):
    groups = source.shape[0]
    half = groups // 2
    fill_parts(source, parts)
    column_sums[...] = jnp.zeros_like(column_sums)

    def step(index, carry):
        out[index, 0] = strip_totals(source[index], parts, index, half + 1, column_sums, True)
        later = index + half
        out[later, 0] = strip_totals(source[later], parts, later, half, column_sums, True)
        return carry

    lax.fori_loop(0, half, step, 0)
    out[:, 0] = out[:, 0] + jnp.sum(column_sums[...], axis=1, keepdims=True)


def totals_kernel(crosses, own, other, own_out, other_out, column_sums, parts):
    groups = own.shape[0]

    @pl.when(crosses[0] == 1)
    def _():
        fill_parts(other, parts)
        column_sums[...] = jnp.zeros_like(column_sums)

        def step(index, carry):
            own_out[index, 0] = strip_totals(own[index], parts, 0, groups, column_sums, False)
            return carry

        lax.fori_loop(0, groups, step, 0)
        other_out[:, 0] = jnp.sum(column_sums[...], axis=1, keepdims=True)

    @pl.when(crosses[0] == 0)
    def _():
        diagonal(own, own_out, column_sums, parts)
        diagonal(other, other_out, column_sums, parts)


def pair_totals(crosses, own, other):
    groups, depth, width = own.shape
    block = pl.BlockSpec((groups, DEPTH, width), lambda w, *_: (0, w, 0))
    line = pl.BlockSpec((groups, 1, 1, width), lambda w, *_: (0, w, 0, 0))
    return pl.pallas_call(
        totals_kernel,
        out_shape=[jax.ShapeDtypeStruct((groups, depth // DEPTH, 1, width), jnp.float32)] * 2,
        grid_spec=pltpu.PrefetchScalarGridSpec(
            num_scalar_prefetch=1,
            grid=(depth // DEPTH,),
            in_specs=[block, block],
            out_specs=[line, line],
            scratch_shapes=[
                pltpu.VMEM((groups, SUBLANES, width), jnp.float32),
                pltpu.VMEM((groups, 4 * DEPTH, width), jnp.float8_e4m3fn),
            ],
        ),
    )(crosses, own, other)


def windows_kernel(tick, prior, out, series):
    width = series.shape[1]
    lead = prior.shape[1] // width
    for row in range(lead):
        series[row : row + 1] = prior[:, row * width : (row + 1) * width]
    for row in range(tick.shape[1] // width):
        series[lead + row : lead + row + 1] = tick[:, row * width : (row + 1) * width]
    for window in range(out.shape[0] * WIN_DEV):
        values = series[window * STRIDE : window * STRIDE + SPAN]
        centred = values - jnp.sum(values, axis=0, keepdims=True) * (1.0 / SPAN)
        squares = jnp.sum(centred * centred, axis=0, keepdims=True)
        scaled = centred * lax.rsqrt(jnp.maximum(squares, FLOOR_SQUARES))
        scaled = jnp.concatenate([scaled, jnp.zeros((DEPTH - SPAN, width), jnp.float32)], axis=0)
        first = window % WIN_DEV * DEPTH
        out[window // WIN_DEV, first : first + DEPTH] = scaled.astype(jnp.bfloat16)


def deliver_kernel(groups, outgoing, own, other, own_send, own_recv, next_send, next_recv, local_sem):
    time = lax.axis_index("tm")
    tile = lax.axis_index("asset")
    next_time, next_tile = cycle_next(time, tile)
    barrier = pltpu.get_barrier_semaphore()
    for step in range(1, groups):
        peer = lax.rem(time + step, groups)
        pl.semaphore_signal(
            barrier, inc=1, device_id=(peer, tile), device_id_type=pl.DeviceIdType.MESH
        )
    pl.semaphore_signal(
        barrier, inc=1, device_id=(time, 1 - tile), device_id_type=pl.DeviceIdType.MESH
    )
    pl.semaphore_wait(barrier, groups)

    def send(step):
        peer = lax.rem(time + step, groups)
        return pltpu.make_async_remote_copy(
            src_ref=outgoing.at[peer],
            dst_ref=own.at[time],
            send_sem=own_send.at[step],
            recv_sem=own_recv.at[step],
            device_id=(peer, tile),
            device_id_type=pl.DeviceIdType.MESH,
        )

    def forward(step):
        source = lax.rem(time - step + groups, groups)
        return pltpu.make_async_remote_copy(
            src_ref=own.at[source],
            dst_ref=other.at[source],
            send_sem=next_send.at[source],
            recv_sem=next_recv.at[source],
            device_id=(next_time, next_tile),
            device_id_type=pl.DeviceIdType.MESH,
        )

    sends = [send(step) for step in range(1, groups)]
    for copy in sends:
        copy.start()
    local = pltpu.make_async_copy(outgoing.at[time], own.at[time], local_sem)
    local.start()
    local.wait()
    forwards = [forward(step) for step in range(groups)]
    forwards[0].start()
    for step in range(1, groups):
        sends[step - 1].wait_recv()
        forwards[step].start()
    for copy in sends:
        copy.wait_send()
    for group in range(groups):
        arrival = pltpu.make_async_remote_copy(
            src_ref=own.at[group],
            dst_ref=other.at[group],
            send_sem=next_send.at[group],
            recv_sem=next_recv.at[group],
            device_id=(next_time, next_tile),
            device_id_type=pl.DeviceIdType.MESH,
        )
        arrival.wait()


def delivered(outgoing):
    groups = outgoing.shape[0]
    vmem = pl.BlockSpec(memory_space=pltpu.VMEM)
    return pl.pallas_call(
        functools.partial(deliver_kernel, groups),
        out_shape=[jax.ShapeDtypeStruct(outgoing.shape, outgoing.dtype)] * 2,
        in_specs=[vmem],
        out_specs=[vmem, vmem],
        scratch_shapes=[pltpu.SemaphoreType.DMA((groups,))] * 4 + [pltpu.SemaphoreType.DMA],
        compiler_params=pltpu.CompilerParams(collective_id=0, has_side_effects=True),
    )(outgoing)


def local_windows(tick_bars, prior_bars):
    groups = lax.axis_size("tm")
    width = ASSETS // (2 * groups)
    ticks, prior = tick_bars.reshape(1, -1), prior_bars.reshape(1, -1)
    if width % LANES:
        series = jnp.concatenate([prior.reshape(-1, width), ticks.reshape(-1, width)], axis=0)
        return window_stack(series).reshape(groups, WIN_DEV * DEPTH, width)
    rows = (ticks.size + prior.size) // width
    return pl.pallas_call(
        windows_kernel,
        out_shape=jax.ShapeDtypeStruct((groups, WIN_DEV * DEPTH, width), jnp.bfloat16),
        scratch_shapes=[pltpu.VMEM((-(-rows // SUBLANES) * SUBLANES, width), jnp.float32)],
    )(ticks, prior)


def retiled(blocks):
    groups, depth, width = blocks.shape
    if width % LANES == 0:
        return blocks
    join = TILE // width
    grouped = blocks.reshape(groups // join, join, depth, width)
    return jnp.transpose(grouped, (0, 2, 1, 3)).reshape(groups // join, depth, TILE)


def shards(tick_bars, prior_bars):
    own, other = delivered(local_windows(tick_bars, prior_bars))
    own, other = retiled(own), retiled(other)
    core = lax.axis_index("tm") % 2
    crosses = (core == lax.axis_index("asset")).astype(jnp.int32).reshape(1)
    own_part, other_part = pair_totals(crosses, own, other)
    own_part = jnp.transpose(own_part[:, :, 0], (1, 0, 2)).reshape(WIN_DEV, -1)
    other_part = jnp.transpose(other_part[:, :, 0], (1, 0, 2)).reshape(WIN_DEV, -1)
    returned = around(other_part, False)
    return (own_part + returned) * (math.sqrt(SPAN) / (ASSETS * PART_SCALE * PART_SCALE))


def solution(mesh):
    in_specs = (P("asset", "tm", None), P("asset", "tm", None))
    out_specs = P("tm", "asset")
    return jax.shard_map(shards, mesh=mesh, in_specs=in_specs, out_specs=out_specs, check_vma=False)
```

profile of v0, /device:TPU:30, one launch (start us, length us, event | category | flops | bytes accessed | tf_op | source)
XLA Modules:
  0.0 77.5 jit_solution(5136868132278588554)
XLA Ops:
  0.0 2.8 %shard_map.28.outgoing = bf16[16,96,256]{2,1,0:T(8,128)(2,1)} custom-call(f32[1,61440]{1,0:T(1,128)} %bitcast.16, f32[1,6400]{1,0:T(1,128)} %bitcast.18), custom_call_target="tpu_custom_call" | custom-call | tf_op jit(solution)/shard_map/pallas_call | solution.py:249
  2.8 28.4 %shard_map.29 = (bf16[16,96,256]{2,1,0:T(8,128)(2,1)}, bf16[16,96,256]{2,1,0:T(8,128)(2,1)}) custom-call(bf16[16,96,256]{2,1,0:T(8,128)(2,1)} %shard_map.28.outgoing), custom_call_target="tpu_custom_call" | custom-call | tf_op jit(solution)/shard_map/pallas_call | solution.py:231
  31.2 40.5 %shard_map.30 = (f32[16,3,1,256]{3,2,1,0:T(1,128)}, f32[16,3,1,256]{3,2,1,0:T(1,128)}) custom-call(s32[1]{0:T(128)} %bitcast.crosses, bf16[16,96,256]{2,1,0:T(8,128)(2,1)} %get-tuple-element.9.own, bf16[16,96,256]{2,1,0:T(8,128)(2,1)} %get-tuple-element.10.other), custom_call_target="tpu_custom_call" | custom-call | tf_op jit(solution)/shard_map/pallas_call | solution.py:133
  71.7 0.8 %copy_bitcast_fusion = (f32[1,3,16,256]{3,2,1,0:T(8,128)S(1)}, f32[1,3,16,256]{3,2,1,0:T(8,128)S(1)}) fusion(f32[16,3,1,256]{3,2,1,0:T(1,128)} %get-tuple-element.12, f32[16,3,1,256]{3,2,1,0:T(1,128)} %get-tuple-element.11), kind=kLoop, calls=%fused_computation.1 | loop fusion | bytes 196608
  72.6 0.0 collective-permute-start
  72.6 4.2 %collective-permute-done = f32[3,4096]{1,0:T(4,128)S(1)} collective-permute-done((f32[3,4096]{1,0:T(4,128)S(1)}, f32[3,4096]{1,0:T(4,128)S(1)}, u32[]{:S(2)}, u32[]{:S(2)}) %collective-permute-start) | collective-permute-done | bytes 49184 | tf_op jit(solution)/shard_map/ppermute | solution.py:40
  76.8 0.7 add_multiply_fusion
  (2 shorter events, 0.1 us)
Async XLA Ops:
  72.6 4.3 %collective-permute-start = (f32[3,4096]{1,0:T(4,128)S(1)}, f32[3,4096]{1,0:T(4,128)S(1)}, u32[]{:S(2)}, u32[]{:S(2)}) collective-permute-start(f32[3,4096]{1,0:T(4,128)S(1)} %bitcast.17), channel_id=1, source_target_pairs={{2,0},{0,1},{3,2},{1,3},{6,4},{4,5},{7,6},{5,7},{10,8},{8,9},{11,1... | collective-permute-start | bytes 147464 | tf_op jit(solution)/shard_map/ppermute | solution.py:40
where the time goes:
time: 77.7 us; the launch traced here: 77.5 us
  Pallas kernels  71.7 us (92%)
  waiting for transfers between devices  4.21 us (5%)
  local copies, waits for them, and re-layouts  0.9 us (1%)
    pallas_call x1, Pallas kernels, pair_totals(): pl.pallas_call(totals_kernel, out_shape=[jax.ShapeDtypeStruct((groups, de...  40.5 us
    pallas_call x1, Pallas kernels, delivered(): pl.pallas_call(functools.partial(deliver_kernel, groups), out_shape=[jax....  28.4 us
    ppermute x1, waiting for transfers between devices, around(): return lax.ppermute(block, ('tm', 'asset'), route)  4.21 us
    pallas_call x1, Pallas kernels, local_windows(): pl.pallas_call(windows_kernel, out_shape=jax.ShapeDtypeStruct((groups, WI...  2.78 us
  transfers between devices with their start and end apart: 1, of which 1 were waited for; matrix products, arithmetic and copies ran while one was open for 0% of the time, Pallas kernels for 0%

commit v1 on v0

--- a/solution.py
+++ b/solution.py
@@ -17,6 +17,7 @@
 TILE = 256
 LANES = 128
 SUBLANES = 8
+CHUNK = 4
 PART_SCALE = 256.0
 
 
@@ -262,7 +263,293 @@
     return jnp.transpose(grouped, (0, 2, 1, 3)).reshape(groups // join, depth, TILE)
 
 
+def tree(terms):
+    terms = list(terms)
+    while len(terms) > 1:
+        paired = [terms[k] + terms[k + 1] for k in range(0, len(terms) - 1, 2)]
+        terms = paired + terms[len(paired) * 2 :]
+    return terms[0]
+
+
+def magnitudes(lhs, rhs):
+    correlation = jnp.dot(lhs, rhs, preferred_element_type=jnp.float32)
+    return jnp.abs(correlation.astype(jnp.bfloat16))
+
+
+def lane_folded(block):
+    return tree(block[:, k : k + LANES] for k in range(0, block.shape[1], LANES))
+
+
+def sublane_folded(block, rows):
+    return tree(block[k : k + rows] for k in range(0, block.shape[0], rows))
+
+
+def add_rows(totals, partial):
+    totals[...] = totals[...] + sublane_folded(partial.astype(jnp.float32).T, SUBLANES)
+
+
+def add_columns(totals, partials):
+    pairs = [tree(partials[k : k + 2]).astype(jnp.float32) for k in range(0, len(partials), 2)]
+    totals[...] = totals[...] + sublane_folded(tree(pairs), SUBLANES)
+
+
+def cross_unit(left, right, row_totals, column_totals):
+    columns = [[] for _ in range(CHUNK)]
+    for u in range(CHUNK):
+        lhs, folded = left[u], []
+        for o in range(CHUNK):
+            block = magnitudes(lhs, right[o])
+            folded.append(lane_folded(block))
+            columns[o].append(sublane_folded(block, 2 * SUBLANES))
+        add_rows(row_totals.at[u], tree(folded))
+    for o in range(CHUNK):
+        add_columns(column_totals.at[o], columns[o])
+
+
+def diagonal_unit(left, right, totals):
+    columns = [[] for _ in range(CHUNK)]
+    for u in range(CHUNK):
+        lhs, folded = left[u], []
+        for o in range(u, CHUNK):
+            block = magnitudes(lhs, right[o])
+            folded.append(lane_folded(block))
+            if o > u:
+                columns[o].append(sublane_folded(block, 2 * SUBLANES))
+        add_rows(totals.at[u], tree(folded))
+    for o in range(1, CHUNK):
+        add_columns(totals.at[o], columns[o])
+
+
+def prepare(series, left, right, window):
+    halves = []
+    for half in range(2):
+        values = series[half, STRIDE * window : STRIDE * window + SPAN]
+        centred = values - jnp.sum(values, axis=0, keepdims=True) * (1.0 / SPAN)
+        squares = jnp.sum(centred * centred, axis=0, keepdims=True)
+        scaled = centred * lax.rsqrt(jnp.maximum(squares, FLOOR_SQUARES))
+        halves.append(scaled.astype(jnp.bfloat16))
+    scaled = jnp.concatenate(halves, axis=1).astype(jnp.float32)
+    pad = jnp.zeros((DEPTH - SPAN, scaled.shape[1]), jnp.float32)
+    high, low = split_parts(jnp.concatenate([scaled, pad], axis=0))
+    high, low = high.astype(jnp.float8_e4m3fn), low.astype(jnp.float8_e4m3fn)
+    right[...] = jnp.concatenate([high, high, low, low], axis=0)
+    left[...] = jnp.concatenate([high, low, high, low], axis=0).T
+
+
+def partner(index, step, size):
+    bit, mirrored = 1, index
+    while bit < size:
+        if step // bit % 2:
+            mirrored = mirrored + bit - 2 * bit * (mirrored // bit % 2)
+        bit *= 2
+    return mirrored
+
+
+def connect_kernel(
+    groups, tick, prior, out, ticks, priors, outgoing, own, other, left, right, totals, sums, back,
+    load_sem, own_send, own_recv, next_send, next_recv, back_send, back_recv,
+):
+    width = 2 * LANES
+    blocks = groups // CHUNK
+    time, tile = lax.axis_index("tm"), lax.axis_index("asset")
+    core = time % 2
+    crosses = 1 - (core + tile) % 2
+    next_time, next_tile = cycle_next(time, tile)
+    along = (1 + core + tile) % 2
+    prev_time, prev_tile = time + (1 - along) * (1 - 2 * core), tile + along * (1 - 2 * tile)
+    block, place = time // CHUNK, time % CHUNK
+    loads = [
+        pltpu.make_async_copy(prior, priors, load_sem.at[0]),
+        pltpu.make_async_copy(tick, ticks, load_sem.at[1]),
+    ]
+    for load in loads:
+        load.start()
+    barrier = pltpu.get_barrier_semaphore()
+    steps = [(s, r) for s in range(blocks) for r in range(CHUNK)]
+
+    def peer(s, r):
+        return partner(block, s, blocks) * CHUNK + partner(place, r, CHUNK)
+
+    for s, r in steps[1:]:
+        pl.semaphore_signal(
+            barrier, inc=1, device_id=(peer(s, r), tile), device_id_type=pl.DeviceIdType.MESH
+        )
+    pl.semaphore_signal(
+        barrier, inc=1, device_id=(time, 1 - tile), device_id_type=pl.DeviceIdType.MESH
+    )
+    for load in loads:
+        load.wait()
+    bars = WIN_DEV * STRIDE
+    for owner in range(groups):
+        first = owner * bars - LEAD
+        early = min(max(-first, 0), bars + LEAD)
+        for half in range(2):
+            if early:
+                begin = 2 * (LEAD - early) + half
+                outgoing[owner, half, :early] = priors[pl.ds(begin, early, stride=2), :]
+            begin = 2 * (first + early) + half
+            late = bars + LEAD - early
+            outgoing[owner, half, early:] = ticks[pl.ds(begin, late, stride=2), :]
+    pl.semaphore_wait(barrier, groups)
+
+    def send(s, r):
+        index = s * CHUNK + r
+        return pltpu.make_async_remote_copy(
+            src_ref=outgoing.at[peer(s, r)],
+            dst_ref=own.at[index],
+            send_sem=own_send.at[index],
+            recv_sem=own_recv.at[index],
+            device_id=(peer(s, r), tile),
+            device_id_type=pl.DeviceIdType.MESH,
+        )
+
+    def forward(s, r):
+        index = s * CHUNK + r
+        return pltpu.make_async_remote_copy(
+            src_ref=own.at[index],
+            dst_ref=other.at[index],
+            send_sem=next_send.at[index],
+            recv_sem=next_recv.at[index],
+            device_id=(next_time, next_tile),
+            device_id_type=pl.DeviceIdType.MESH,
+        )
+
+    local = pltpu.make_async_copy(outgoing.at[time], own.at[0], load_sem.at[0])
+    local.start()
+    sends = {step: send(*step) for step in steps[1:]}
+    for step in steps[1:]:
+        sends[step].start()
+    forwards = {step: forward(*step) for step in steps}
+
+    totals[...] = jnp.zeros_like(totals)
+
+    def pass_on(s):
+        for r in range(CHUNK):
+            if s or r:
+                sends[s, r].wait_recv()
+            else:
+                local.wait()
+            forwards[s, r].start()
+
+    def units(s):
+        for r in range(CHUNK):
+            forwards[s, r].wait_recv()
+
+        def fill(i, carry):
+            group = s * CHUNK + i
+            for window in range(WIN_DEV):
+                prepare(own.at[group], left.at[0, window, group], right.at[0, window, group], window)
+                prepare(other.at[group], left.at[1, window, group], right.at[1, window, group], window)
+            return carry
+
+        lax.fori_loop(0, CHUNK, fill, 0)
+
+        def chunk_of(ref, which, window, k):
+            return ref.at[which, window, pl.ds(k * CHUNK, CHUNK)]
+
+        def pair(k, carry):
+            for window in range(WIN_DEV):
+                for side in range(2):
+                    row_set, column_set = (1 - crosses, 1) if side else (0, crosses)
+                    row_chunk, column_chunk = (k, s) if side else (s, k)
+                    cross_unit(
+                        chunk_of(left, row_set, window, row_chunk),
+                        chunk_of(right, column_set, window, column_chunk),
+                        chunk_of(totals, row_set, window, row_chunk),
+                        chunk_of(totals, column_set, window, column_chunk),
+                    )
+            return carry
+
+        lax.fori_loop(0, s, pair, 0)
+
+        @pl.when(crosses == 1)
+        def _():
+            for window in range(WIN_DEV):
+                cross_unit(
+                    chunk_of(left, 0, window, s),
+                    chunk_of(right, 1, window, s),
+                    chunk_of(totals, 0, window, s),
+                    chunk_of(totals, 1, window, s),
+                )
+
+        @pl.when(crosses == 0)
+        def _():
+            for window in range(WIN_DEV):
+                for which in range(2):
+                    diagonal_unit(
+                        chunk_of(left, which, window, s),
+                        chunk_of(right, which, window, s),
+                        chunk_of(totals, which, window, s),
+                    )
+
+    pass_on(0)
+    pass_on(1)
+    units(0)
+    pass_on(2)
+    units(1)
+    pass_on(3)
+    units(2)
+    units(3)
+
+    sums[...] = jnp.sum(totals[1], axis=2, keepdims=True)
+    returned = pltpu.make_async_remote_copy(
+        src_ref=sums,
+        dst_ref=back,
+        send_sem=back_send,
+        recv_sem=back_recv,
+        device_id=(prev_time, prev_tile),
+        device_id_type=pl.DeviceIdType.MESH,
+    )
+    returned.start()
+    for step in steps[1:]:
+        sends[step].wait_send()
+    for step in steps:
+        forwards[step].wait_send()
+    mine = jnp.sum(totals[0], axis=2, keepdims=True)
+    returned.wait()
+    scale = math.sqrt(SPAN) / (ASSETS * PART_SCALE * PART_SCALE)
+    mine = (mine + back[...]) * scale
+    for s, r in steps:
+        lanes = pl.ds(pl.multiple_of(peer(s, r) * width, LANES), width)
+        for window in range(WIN_DEV):
+            out[window : window + 1, lanes] = mine[window, s * CHUNK + r]
+
+
+def connected(tick_bars, prior_bars):
+    groups = lax.axis_size("tm")
+    ticks, prior = tick_bars.reshape(-1, LANES), prior_bars.reshape(-1, LANES)
+    width = 2 * LANES
+    block = (groups, 2, WIN_DEV * STRIDE + LEAD, LANES)
+    dma = pltpu.SemaphoreType.DMA
+    f8 = jnp.float8_e4m3fn
+    return pl.pallas_call(
+        functools.partial(connect_kernel, groups),
+        out_shape=jax.ShapeDtypeStruct((WIN_DEV, groups * width), jnp.float32),
+        in_specs=[pl.BlockSpec(memory_space=pl.ANY)] * 2,
+        out_specs=pl.BlockSpec(memory_space=pltpu.VMEM),
+        scratch_shapes=[
+            pltpu.VMEM(ticks.shape, jnp.float32),
+            pltpu.VMEM(prior.shape, jnp.float32),
+            pltpu.VMEM(block, jnp.float32),
+            pltpu.VMEM(block, jnp.float32),
+            pltpu.VMEM(block, jnp.float32),
+            pltpu.VMEM((2, WIN_DEV, groups, width, 4 * DEPTH), f8),
+            pltpu.VMEM((2, WIN_DEV, groups, 4 * DEPTH, width), f8),
+            pltpu.VMEM((2, WIN_DEV, groups, SUBLANES, width), jnp.float32),
+            pltpu.VMEM((WIN_DEV, groups, 1, width), jnp.float32),
+            pltpu.VMEM((WIN_DEV, groups, 1, width), jnp.float32),
+            dma((2,)), dma((groups,)), dma((groups,)), dma((groups,)), dma((groups,)), dma, dma,
+        ],
+        compiler_params=pltpu.CompilerParams(
+            collective_id=1, has_side_effects=True, vmem_limit_bytes=60 * 1024 * 1024
+        ),
+    )(ticks, prior)
+
+
 def shards(tick_bars, prior_bars):
+    groups = lax.axis_size("tm")
+    if groups == 4 * CHUNK and ASSETS == groups * 4 * LANES:
+        return connected(tick_bars, prior_bars)
     own, other = delivered(local_windows(tick_bars, prior_bars))
     own, other = retiled(own), retiled(other)
     core = lax.axis_index("tm") % 2

time: 77.7 us -> 47.1 us (0.61)
  the two profiles are of different devices: /device:TPU:30 before, /device:TPU:1 now
where the time goes in v1:
time: 47.1 us; the launch traced here: 46.9 us
  Pallas kernels  44 us (93%)
  local copies, waits for them, and re-layouts  1.48 us (3%)
  other arithmetic  1.41 us (3%)
    pallas_call x1, Pallas kernels, connected(): pl.pallas_call(functools.partial(connect_kernel, groups), out_shape=jax.S...  44 us
    unnamed x1, local copies, waits for them, and re-layouts  1.48 us
    unnamed x1, other arithmetic  1.41 us

profile of v1, /device:TPU:1, one launch (start us, length us, event | category | flops | bytes accessed | tf_op | source)
XLA Modules:
  0.0 46.9 jit_solution(14250931015843362505)
XLA Ops:
  0.0 1.4 %reduce = f32[6400]{0:T(1024)} reduce(f32[1,1,6400]{2,1,0:T(1,128)} %param.3, f32[]{:T(128)} %constant.2), dimensions={0,1}, to_apply=%param.3.reduce_sub_computation | reduce | bytes 51204 | tf_op args[1]
  1.4 44.0 %shard_map.28 = f32[3,4096]{1,0:T(4,128)} custom-call(f32[480,128]{1,0:T(8,128)} %bitcast.2, f32[50,128]{1,0:T(8,128)} %bitcast.3), custom_call_target="tpu_custom_call" | custom-call | tf_op jit(solution)/shard_map/pallas_call | solution.py:525
  45.4 1.5 %copy.4 = f32[3,4096]{1,0:T(4,128)} copy(f32[3,4096]{1,0:T(4,128)} %shard_map.28) | data formatting | bytes 98304
